TPU v7x, 32 devices: a whole 2x2x4 slice. The times are simulated.
32 devices in a mesh: section: 2 (over core), dp: 4 (over y, x), tensor: 4 (over z).
Axes of the slice: x: 2, y: 2, z: 4, core: 2. Of those that a mesh axis runs over, the one named last changes fastest.
Arguments:
- tokens_in: bfloat16 [512, 8192], P('dp', ('section', 'tensor')), may hold values from -70 to 70
- gain_attn: bfloat16 [8192], replicated, may hold values from 0.5 to 1.5
- w_query: bfloat16 [8192, 8192], P(None, ('section', 'tensor')), may hold values from -6 to 6
- w_keyval: bfloat16 [8192, 2048], P(None, ('section', 'tensor')), may hold values from -0.0625 to 0.0625
- w_out: bfloat16 [8192, 8192], P(('section', 'tensor')), may hold values from -0.0625 to 0.0625
- gain_mlp: bfloat16 [8192], replicated, may hold values from 0.5 to 1.5
- w_gate: bfloat16 [8192, 16384], P('dp', ('section', 'tensor')), may hold values from -0.0625 to 0.0625
- w_up: bfloat16 [8192, 16384], P('dp', ('section', 'tensor')), may hold values from -0.0625 to 0.0625
- w_down: bfloat16 [16384, 8192], P(('section', 'tensor'), 'dp'), may hold values from -0.046875 to 0.046875
Outputs:
- layer_out: bfloat16 [512, 8192], P(('section', 'tensor'), 'dp')
All inputs are finite; a program needn't handle non-finite values.
Results may differ from a plain program's by a relative error of at most 0.0068.
Values may be sent and summed in bfloat16 or wider, within the bound.
A program may use at most 128 MiB of HBM per device.

v0:
```python
import jax
import jax.numpy as jnp
from jax import lax
from jax.sharding import PartitionSpec as P

H = 64
KVH = 8
HD = 128
EPS = 1e-05
THETA = 10000.0


def rms_scale(row_data, gain_row):
    values = row_data.astype(jnp.float32)
    factor = lax.rsqrt(jnp.mean(values * values, axis=-1, keepdims=True) + EPS)
    return (values * factor * gain_row.astype(jnp.float32)).astype(jnp.bfloat16)


def rotary(values, positions):
    half_dim = values.shape[-1] // 2
    frequency = THETA ** (-jnp.arange(half_dim, dtype=jnp.float32) * 2.0 / values.shape[-1])
    angles = positions.astype(jnp.float32)[:, None] * frequency[None, :]
    cosine = jnp.cos(angles)[:, None, :]
    sine_part = jnp.sin(angles)[:, None, :]
    first_half = values[..., :half_dim]
    second = values[..., half_dim:]
    return jnp.concatenate(
        [first_half * cosine - second * sine_part, second * cosine + first_half * sine_part],
        axis=-1,
    )


def shards(tokens_in, gain_attn, w_query, w_keyval, w_out, gain_mlp, w_gate, w_up, w_down):
    group_count = lax.axis_size(("section", "tensor"))
    group_index = lax.axis_index(("section", "tensor"))
    data_index = lax.axis_index("dp")
    local_rows = tokens_in.shape[0]
    full_rows = lax.all_gather(tokens_in, ("section", "tensor"), axis=1, tiled=True)
    normed_attn = rms_scale(full_rows, gain_attn)
    heads_dev = w_query.shape[1] // HD
    group_size = H // KVH
    kv_dev = max(1, heads_dev // group_size)
    positions_local = data_index * local_rows + jnp.arange(local_rows, dtype=jnp.int32)
    query_proj = jnp.dot(normed_attn, w_query, preferred_element_type=jnp.float32)
    query_rot = rotary(query_proj.reshape(local_rows, heads_dev, HD), positions_local).astype(
        jnp.bfloat16
    )
    keyval_part = jnp.dot(normed_attn, w_keyval, preferred_element_type=jnp.float32).astype(
        jnp.bfloat16
    )
    keyval_rows = lax.all_gather(keyval_part, ("section", "tensor"), axis=1, tiled=True)
    first_kv = group_index * heads_dev // group_size
    key_cols = lax.dynamic_slice_in_dim(keyval_rows, first_kv * HD, kv_dev * HD, 1)
    value_cols = lax.dynamic_slice_in_dim(keyval_rows, KVH * HD + first_kv * HD, kv_dev * HD, 1)
    needed = jnp.concatenate([key_cols, value_cols], axis=1)
    kv_all = lax.all_gather(needed, "dp", axis=0, tiled=True)
    total_rows = kv_all.shape[0]
    key_pos = jnp.arange(total_rows, dtype=jnp.int32)
    key_rot = rotary(
        kv_all[:, : kv_dev * HD].astype(jnp.float32).reshape(total_rows, kv_dev, HD), key_pos
    ).astype(jnp.bfloat16)
    value_all = kv_all[:, kv_dev * HD :].reshape(total_rows, kv_dev, HD)
    query_grp = query_rot.reshape(local_rows, kv_dev, heads_dev // kv_dev, HD)
    scores = jnp.einsum(
        "rkgd,skd->kgrs", query_grp, key_rot, preferred_element_type=jnp.float32
    ) * HD ** (-0.5)
    allowed = key_pos[None, :] <= positions_local[:, None]
    scores = jnp.where(allowed[None, None, :, :], scores, -1e30)
    row_peak = jnp.max(scores, axis=-1, keepdims=True)
    expo_rows = jnp.exp(scores - row_peak)
    prob_rows = (expo_rows / jnp.sum(expo_rows, axis=-1, keepdims=True)).astype(jnp.bfloat16)
    attended = jnp.einsum(
        "kgrs,skd->rkgd", prob_rows, value_all, preferred_element_type=jnp.float32
    )
    attended = attended.astype(jnp.bfloat16).reshape(local_rows, heads_dev * HD)
    head_terms = jnp.dot(attended, w_out, preferred_element_type=jnp.float32)
    summed = lax.psum(head_terms, ("section", "tensor"))
    mid_full = (full_rows.astype(jnp.float32) + summed).astype(jnp.bfloat16)
    normed_mlp = rms_scale(mid_full, gain_mlp)
    mid_cols, norm_cols = (
        lax.all_to_all(mid_full, "dp", split_axis=1, concat_axis=0, tiled=True),
        lax.all_to_all(normed_mlp, "dp", split_axis=1, concat_axis=0, tiled=True),
    )
    hidden_width = w_gate.shape[1]
    row_block = norm_cols
    gate_block = jnp.dot(row_block, w_gate, preferred_element_type=jnp.float32)
    up_block = jnp.dot(row_block, w_up, preferred_element_type=jnp.float32)
    gate_both = lax.psum_scatter(
        jnp.concatenate([gate_block, up_block], axis=1), "dp", scatter_dimension=0, tiled=True
    )
    hidden_part = (jax.nn.silu(gate_both[:, :hidden_width]) * gate_both[:, hidden_width:]).astype(
        jnp.bfloat16
    )
    hidden_all = lax.all_gather(hidden_part, "dp", axis=0, tiled=True)
    out_rows = hidden_all.shape[0] // group_count
    row_block = hidden_all
    down_part = lax.psum_scatter(
        jnp.dot(row_block, w_down, preferred_element_type=jnp.float32),
        ("section", "tensor"),
        scatter_dimension=0,
        tiled=True,
    )
    resid_rows = lax.dynamic_slice_in_dim(mid_cols, group_index * out_rows, out_rows, 0)
    return (resid_rows.astype(jnp.float32) + down_part).astype(jnp.bfloat16)


def solution(mesh):
    placed = (
        P("dp", ("section", "tensor")),
        P(),
        P(None, ("section", "tensor")),
        P(None, ("section", "tensor")),
        P(("section", "tensor"), None),
        P(),
        P("dp", ("section", "tensor")),
        P("dp", ("section", "tensor")),
        P(("section", "tensor"), "dp"),
    )
    return jax.shard_map(
        shards,
        mesh=mesh,
        in_specs=placed,
        out_specs=P(("section", "tensor"), "dp"),
        check_vma=False,
    )
```

profile of v0, /device:TPU:0, one launch (start us, length us, event | category | flops | bytes accessed | tf_op | source)
XLA Modules:
  0.0 471.4 jit_solution(17559355887173237044)
XLA Ops:
  8.5 32.4 %all-gather.3.cloned.1.call-done = bf16[128,8192]{1,0:T(8,128)(2,1)} async-done(((bf16[128,1024]{1,0:T(8,128)(2,1)}), bf16[128,8192]{1,0:T(8,128)(2,1)}) %all-gather.3.cloned.1.call-update) | async-done | bytes 2097168 | tf_op jit(solution)/shard_map/all_gather | solution.py:38
  40.8 2.1 fusion.3
  42.9 3.7 convolution_convert_fusion.1
  46.7 26.2 %all_gather.13 = bf16[128,2048]{1,0:T(8,128)(2,1)S(1)} all-gather(bf16[128,256]{1,0:T(8,128)(2,1)S(1)} %convolution_convert_fusion.1), channel_id=1, replica_groups=mesh['section'=2,'dp'=4,'tensor'=4] {'section','tensor'}, dimensions={1}, use_global_device_ids=true | all-gather | bytes 589824 | tf_op jit(solution)/shard_map/all_gather | solution.py:51
  72.9 9.0 %all_gather.14 = bf16[512,256]{1,0:T(8,128)(2,1)S(1)} all-gather(bf16[128,256]{1,0:T(8,128)(2,1)S(1)} %pad_maximum_fusion.1), channel_id=1, replica_groups=mesh['section'=2,'dp'=4,'tensor'=4] {'dp'}, dimensions={0}, use_global_device_ids=true | all-gather | bytes 327680 | tf_op jit(solution)/shard_map/all_gather | solution.py:56
  81.9 8.4 %convolution_bitcast_fusion = f32[16,8,8,128]{3,1,2,0:T(8,128)S(1)} fusion(bf16[8192,1024]{1,0:T(8,128)(2,1)} %param.11, bf16[128,8192]{1,0:T(8,128)(2,1)S(1)} %copy-done, f32[8192]{0:T(1024)S(1)} %convert_element_type.75, f32[128]{0:T(128)S(1)} %add_rsqrt_fusion.1), kind=kOutput, calls=%fused_computation.19 | convolution fusion | flops 2151677952 | bytes 19431936 | tf_op jit(solution)/shard_map/dot_general | solution.py:44
  90.7 1.2 fusion.27
  93.6 0.7 slice-done.3
  94.3 4.8 %fusion.33 = f32[128,8192]{1,0:T(8,128)} fusion(bf16[128,1024]{0,1:T(8,128)(2,1)S(1)} %bitcast.66, bf16[1024,8192]{1,0:T(8,128)(2,1)S(1)} %bitcast.58), kind=kOutput, calls=%fused_computation.64 | convolution fusion | flops 2147483648 | bytes 21233664 | tf_op jit(solution)/shard_map/dot_general | solution.py:76
  99.9 94.9 %all-reduce.2.cloned.1.call-done = f32[128,8192]{1,0:T(8,128)} async-done(((f32[128,8192]{1,0:T(8,128)}), f32[128,8192]{1,0:T(8,128)}) %all-reduce.2.cloned.1.call-update) | async-done | bytes 4194320 | tf_op jit(solution)/shard_map/psum | solution.py:77
  194.8 3.7 fusion
  199.4 28.8 %all_to_all.38 = bf16[128,4,2048]{2,0,1:T(8,128)(2,1)S(1)} all-to-all(bf16[128,4,2048]{2,0,1:T(8,128)(2,1)S(1)} %bitcast.61), channel_id=1, replica_groups=mesh['section'=2,'dp'=4,'tensor'=4] {'dp'}, dimensions={1} | all-to-all | bytes 4194304 | tf_op jit(solution)/shard_map/all_to_all | solution.py:82
  228.3 4.6 fusion.35
  232.9 4.6 fusion.34
  237.5 3.8 pad_maximum_fusion
  241.4 85.1 %reduce-scatter.3.cloned.1.call-done = f32[128,4096]{1,0:T(8,128)} async-done(((f32[512,4096]{1,0:T(8,128)}), f32[128,4096]{1,0:T(8,128)}) %reduce-scatter.3.cloned.1.call-update) | async-done | bytes 2097168 | tf_op jit(solution)/shard_map/reduce_scatter | solution.py:88
  326.5 2.6 fusion.8
  329.2 35.3 %all-gather.5.cloned.1.call-done = bf16[512,2048]{1,0:T(8,128)(2,1)} async-done(((bf16[128,2048]{1,0:T(8,128)(2,1)}), bf16[512,2048]{1,0:T(8,128)(2,1)}) %all-gather.5.cloned.1.call-update) | async-done | bytes 2097168 | tf_op jit(solution)/shard_map/all_gather | solution.py:94
  364.5 10.5 %fusion.36 = f32[512,2048]{1,0:T(8,128)} fusion(bf16[512,2048]{1,0:T(8,128)(2,1)} %all-gather.5.cloned.1.call-done, bf16[2048,2048]{1,0:T(8,128)(2,1)} %param.17), kind=kOutput, calls=%fused_computation.67 | convolution fusion | flops 4294967296 | bytes 14680064 | tf_op jit(solution)/shard_map/dot_general | solution.py:98
  374.9 1.5 copy.42
  376.4 3.6 all-to-all-start
  380.0 24.9 %all-to-all-done = bf16[128,4,2048]{2,0,1:T(8,128)(2,1)S(1)} async-done(((bf16[128,4,2048]{2,0,1:T(8,128)(2,1)}), bf16[128,4,2048]{2,0,1:T(8,128)(2,1)S(1)}, u32[]{:S(2)}, u32[]{:S(2)}) %all-to-all-start) | async-done | bytes 2097184 | tf_op jit(solution)/shard_map/all_to_all | solution.py:81
  405.0 58.1 %reduce-scatter.5.cloned.1.call-done = f32[64,2048]{1,0:T(8,128)} async-done(((f32[512,2048]{1,0:T(8,128)}), f32[64,2048]{1,0:T(8,128)}) %reduce-scatter.5.cloned.1.call-update) | async-done | bytes 524304 | tf_op jit(solution)/shard_map/reduce_scatter | solution.py:97
  463.1 1.8 add_convert_fusion
  (53 shorter events, 5.6 us)
Async XLA Ops:
  6.5 34.3 %all-gather.3.cloned.1.call-start = ((), (), s32[]{:S(2)}) async-start(), calls=%async_computation.4 | async-start | bytes 2359296 | tf_op jit(solution)/shard_map/all_gather | solution.py:38
  7.3 187.5 %all-reduce.2.cloned.1.call-start = ((), (), s32[]{:S(2)}) async-start(), calls=%async_computation.5 | async-start | bytes 8388608 | tf_op jit(solution)/shard_map/psum | solution.py:77
  42.9 39.0 %copy-start = (bf16[128,8192]{1,0:T(8,128)(2,1)S(1)}, bf16[128,8192]{1,0:T(8,128)(2,1)}, u32[]{:S(2)}) copy-start(bf16[128,8192]{1,0:T(8,128)(2,1)} %all-gather.3.cloned.1.call-done) | copy-start | bytes 6291460
  81.9 11.6 %slice-start = ((s8[16777216]{0:T(1024)(128)(4,1)}), s8[4194304]{0:T(1024)(128)(4,1)S(1)}, s32[]{:S(2)}) async-start(s8[16777216]{0:T(1024)(128)(4,1)} %bitcast.57), calls=%async_computation.9 | async-start | bytes 8388608
  81.9 11.6 %slice-start.1 = ((s8[16777216]{0:T(1024)(128)(4,1)}), s8[4194304]{0:T(1024)(128)(4,1)S(1)}, s32[]{:S(2)}) async-start(s8[16777216]{0:T(1024)(128)(4,1)} %bitcast.57), calls=%async_computation.10 | async-start | bytes 8388608
  81.9 11.6 %slice-start.2 = ((s8[16777216]{0:T(1024)(128)(4,1)}), s8[4194304]{0:T(1024)(128)(4,1)S(1)}, s32[]{:S(2)}) async-start(s8[16777216]{0:T(1024)(128)(4,1)} %bitcast.57), calls=%async_computation.11 | async-start | bytes 8388608
  92.1 2.2 slice-start.3
  99.1 0.7 copy-start.1
  99.2 227.3 %reduce-scatter.3.cloned.1.call-start = ((), (), s32[]{:S(2)}) async-start(), calls=%async_computation.6 | async-start | bytes 10485760 | tf_op jit(solution)/shard_map/reduce_scatter | solution.py:88
  194.8 33.5 %slice-start.4 = ((s8[8388608]{0:T(1024)(128)(4,1)}), s8[4194304]{0:T(1024)(128)(4,1)S(1)}, s32[]{:S(2)}) async-start(s8[8388608]{0:T(1024)(128)(4,1)} %bitcast.67), calls=%async_computation.13 | async-start | bytes 8388608
  198.5 29.8 %slice-start.5 = ((s8[8388608]{0:T(1024)(128)(4,1)}), s8[4194304]{0:T(1024)(128)(4,1)S(1)}, s32[]{:S(2)}) async-start(s8[8388608]{0:T(1024)(128)(4,1)} %bitcast.67), calls=%async_computation.14 | async-start | bytes 8388608
  199.4 33.5 %slice-start.6 = ((s8[8388608]{0:T(1024)(128)(4,1)}), s8[4194304]{0:T(1024)(128)(4,1)S(1)}, s32[]{:S(2)}) async-start(s8[8388608]{0:T(1024)(128)(4,1)} %bitcast.69), calls=%async_computation.15 | async-start | bytes 8388608
  228.3 4.6 slice-start.7
  241.3 123.2 %all-gather.5.cloned.1.call-start = ((), (), s32[]{:S(2)}) async-start(), calls=%async_computation.7 | async-start | bytes 2621440 | tf_op jit(solution)/shard_map/all_gather | solution.py:94
  329.1 133.9 %reduce-scatter.5.cloned.1.call-start = ((), (), s32[]{:S(2)}) async-start(), calls=%async_computation.8 | async-start | bytes 4718592 | tf_op jit(solution)/shard_map/reduce_scatter | solution.py:97
  376.4 28.6 %all-to-all-start = ((bf16[128,4,2048]{2,0,1:T(8,128)(2,1)}), bf16[128,4,2048]{2,0,1:T(8,128)(2,1)S(1)}, u32[]{:S(2)}, u32[]{:S(2)}) async-start(bf16[128,4,2048]{2,0,1:T(8,128)(2,1)} %bitcast.59), calls=%async_computation | async-start | bytes 4194304 | tf_op jit(solution)/shard_map/all_to_all | solution.py:81
Sparse Core Ops, SparseCore 0:
  8.9 31.8 all-gather.2
  99.3 95.4 all-reduce.1
  241.4 85.0 reduce-scatter.2
  329.3 35.1 all-gather.4
  375.1 87.9 reduce-scatter.4
where the time goes:
time: 472 us; the launch traced here: 471 us
  waiting for transfers between devices  332 us (70%)
  blocking collectives  64 us (14%)
  matrix products  37.7 us (8%)
  other arithmetic  17.5 us (4%)
  between operations  13.5 us (3%)
    psum x1, waiting for transfers between devices, shards(): summed = lax.psum(head_terms, ('section', 'tensor'))  94.9 us
    reduce_scatter x1, waiting for transfers between devices, shards(): lax.psum_scatter(jnp.concatenate([gate_block, up_block], axis=1), 'dp', s...  85.1 us
    reduce_scatter x1, waiting for transfers between devices, shards(): lax.psum_scatter(jnp.dot(row_block, w_down, preferred_element_type=jnp.fl...  58.1 us
    all_gather x1, waiting for transfers between devices, shards(): hidden_all = lax.all_gather(hidden_part, 'dp', axis=0, tiled=True)  35.3 us
    all_gather x1, waiting for transfers between devices, shards(): lax.all_gather(tokens_in, ('section', 'tensor'), axis=1, tiled=True)  32.4 us
    all_to_all x1, blocking collectives, shards(): lax.all_to_all(normed_mlp, 'dp', split_axis=1, concat_axis=0, tiled=True)  28.8 us
    all_gather x1, blocking collectives, shards(): lax.all_gather(keyval_part, ('section', 'tensor'), axis=1, tiled=True)  26.2 us
    all_to_all x1, waiting for transfers between devices, shards(): lax.all_to_all(mid_full, 'dp', split_axis=1, concat_axis=0, tiled=True)  24.9 us
  transfers between devices with their start and end apart: 6, of which 6 were waited for; matrix products, arithmetic and copies ran while one was open for 1% of the time, Pallas kernels for 0%

commit v1 on v0

--- a/solution.py
+++ b/solution.py
@@ -2,6 +2,7 @@
 import jax.numpy as jnp
 from jax import lax
 from jax.sharding import PartitionSpec as P
+from jax.lax import psum
 
 H = 64
 KVH = 8
@@ -74,7 +75,7 @@
     )
     attended = attended.astype(jnp.bfloat16).reshape(local_rows, heads_dev * HD)
     head_terms = jnp.dot(attended, w_out, preferred_element_type=jnp.float32)
-    summed = lax.psum(head_terms, ("section", "tensor"))
+    summed = psum(psum(head_terms, "tensor"), "section")
     mid_full = (full_rows.astype(jnp.float32) + summed).astype(jnp.bfloat16)
     normed_mlp = rms_scale(mid_full, gain_mlp)
     mid_cols, norm_cols = (

time: 472 us -> 562 us (1.19)
  waiting for transfers between devices: 332 us -> 421 us
    psum x1 -> x2, waiting for transfers between devices: 94.9 us -> 184 us  [shards(): summed = psum(psum(head_terms, 'tensor'), 'section')]
  transfers between devices with their start and end apart: 6 -> 7, of which waited for: 6 -> 7; matrix products, arithmetic and copies ran while one was open for 1% -> 0% of each run, Pallas kernels for 0% -> 0%
where the time goes in v1:
time: 562 us
  waiting for transfers between devices  421 us (75%)
  blocking collectives  65 us (12%)
  matrix products  37.7 us (7%)
  other arithmetic  17.5 us (3%)
  between operations  13.8 us (2%)
    psum x2, waiting for transfers between devices, shards(): summed = psum(psum(head_terms, 'tensor'), 'section')  184 us
    reduce_scatter x1, waiting for transfers between devices, shards(): lax.psum_scatter(jnp.concatenate([gate_block, up_block], axis=1), 'dp', s...  85.8 us
    reduce_scatter x1, waiting for transfers between devices, shards(): lax.psum_scatter(jnp.dot(row_block, w_down, preferred_element_type=jnp.fl...  58.1 us
    all_gather x1, waiting for transfers between devices, shards(): hidden_all = lax.all_gather(hidden_part, 'dp', axis=0, tiled=True)  35.3 us
    all_gather x1, waiting for transfers between devices, shards(): lax.all_gather(tokens_in, ('section', 'tensor'), axis=1, tiled=True)  32.4 us
    all_to_all x1, blocking collectives, shards(): lax.all_to_all(normed_mlp, 'dp', split_axis=1, concat_axis=0, tiled=True)  29.8 us
    all_gather x1, blocking collectives, shards(): lax.all_gather(keyval_part, ('section', 'tensor'), axis=1, tiled=True)  26.2 us
    all_to_all x1, waiting for transfers between devices, shards(): lax.all_to_all(mid_full, 'dp', split_axis=1, concat_axis=0, tiled=True)  24.9 us
  transfers between devices with their start and end apart: 7, of which 7 were waited for; matrix products, arithmetic and copies ran while one was open for 0% of the time, Pallas kernels for 0%

profile of v1, /device:TPU:0, one launch (start us, length us, event | category | flops | bytes accessed | tf_op | source)
XLA Modules:
  0.0 561.7 jit_solution(19320388560933179)
XLA Ops:
  8.5 32.4 %all-gather.3.cloned.1.call-done = bf16[128,8192]{1,0:T(8,128)(2,1)} async-done(((bf16[128,1024]{1,0:T(8,128)(2,1)}), bf16[128,8192]{1,0:T(8,128)(2,1)}) %all-gather.3.cloned.1.call-update) | async-done | bytes 2097168 | tf_op jit(solution)/shard_map/all_gather | solution.py:39
  40.8 2.1 fusion.3
  42.9 3.7 convolution_convert_fusion.1
  46.7 26.2 %all_gather.13 = bf16[128,2048]{1,0:T(8,128)(2,1)S(1)} all-gather(bf16[128,256]{1,0:T(8,128)(2,1)S(1)} %convolution_convert_fusion.1), channel_id=1, replica_groups=mesh['section'=2,'dp'=4,'tensor'=4] {'section','tensor'}, dimensions={1}, use_global_device_ids=true | all-gather | bytes 589824 | tf_op jit(solution)/shard_map/all_gather | solution.py:52
  72.9 9.0 %all_gather.14 = bf16[512,256]{1,0:T(8,128)(2,1)S(1)} all-gather(bf16[128,256]{1,0:T(8,128)(2,1)S(1)} %pad_maximum_fusion.1), channel_id=1, replica_groups=mesh['section'=2,'dp'=4,'tensor'=4] {'dp'}, dimensions={0}, use_global_device_ids=true | all-gather | bytes 327680 | tf_op jit(solution)/shard_map/all_gather | solution.py:57
  81.9 8.4 %convolution_bitcast_fusion = f32[16,8,8,128]{3,1,2,0:T(8,128)S(1)} fusion(bf16[8192,1024]{1,0:T(8,128)(2,1)} %param.11, bf16[128,8192]{1,0:T(8,128)(2,1)S(1)} %copy-done, f32[8192]{0:T(1024)S(1)} %convert_element_type.75, f32[128]{0:T(128)S(1)} %add_rsqrt_fusion.1), kind=kOutput, calls=%fused_computation.19 | convolution fusion | flops 2151677952 | bytes 19431936 | tf_op jit(solution)/shard_map/dot_general | solution.py:45
  90.7 1.2 fusion.27
  94.3 4.8 fusion.33
  99.2 154.1 %all-reduce.3.cloned.1.call-done = f32[128,8192]{1,0:T(8,128)} async-done(((f32[128,8192]{1,0:T(8,128)}), f32[128,8192]{1,0:T(8,128)}) %all-reduce.3.cloned.1.call-update) | async-done | bytes 4194320 | tf_op jit(solution)/shard_map/psum | solution.py:78
  253.4 29.6 %all-reduce.5.cloned.1.call-done = f32[128,8192]{1,0:T(8,128)} async-done(((f32[128,8192]{1,0:T(8,128)}), f32[128,8192]{1,0:T(8,128)}) %all-reduce.5.cloned.1.call-update) | async-done | bytes 4194320 | tf_op jit(solution)/shard_map/psum | solution.py:78
  283.0 3.7 fusion
  287.7 29.8 %all_to_all.38 = bf16[128,4,2048]{2,0,1:T(8,128)(2,1)S(1)} all-to-all(bf16[128,4,2048]{2,0,1:T(8,128)(2,1)S(1)} %bitcast.61), channel_id=1, replica_groups=mesh['section'=2,'dp'=4,'tensor'=4] {'dp'}, dimensions={1} | all-to-all | bytes 4194304 | tf_op jit(solution)/shard_map/all_to_all | solution.py:83
  317.5 4.6 fusion.35
  322.1 4.6 fusion.34
  326.7 3.8 pad_maximum_fusion
  330.6 85.8 %reduce-scatter.3.cloned.1.call-done = f32[128,4096]{1,0:T(8,128)} async-done(((f32[512,4096]{1,0:T(8,128)}), f32[128,4096]{1,0:T(8,128)}) %reduce-scatter.3.cloned.1.call-update) | async-done | bytes 2097168 | tf_op jit(solution)/shard_map/reduce_scatter | solution.py:89
  416.4 2.6 fusion.8
  419.1 35.3 %all-gather.5.cloned.1.call-done = bf16[512,2048]{1,0:T(8,128)(2,1)} async-done(((bf16[128,2048]{1,0:T(8,128)(2,1)}), bf16[512,2048]{1,0:T(8,128)(2,1)}) %all-gather.5.cloned.1.call-update) | async-done | bytes 2097168 | tf_op jit(solution)/shard_map/all_gather | solution.py:95
  454.4 10.5 %fusion.36 = f32[512,2048]{1,0:T(8,128)} fusion(bf16[512,2048]{1,0:T(8,128)(2,1)} %all-gather.5.cloned.1.call-done, bf16[2048,2048]{1,0:T(8,128)(2,1)} %param.17), kind=kOutput, calls=%fused_computation.67 | convolution fusion | flops 4294967296 | bytes 14680064 | tf_op jit(solution)/shard_map/dot_general | solution.py:99
  464.9 1.5 copy.42
  466.4 3.6 all-to-all-start
  470.0 24.9 %all-to-all-done = bf16[128,4,2048]{2,0,1:T(8,128)(2,1)S(1)} async-done(((bf16[128,4,2048]{2,0,1:T(8,128)(2,1)}), bf16[128,4,2048]{2,0,1:T(8,128)(2,1)S(1)}, u32[]{:S(2)}, u32[]{:S(2)}) %all-to-all-start) | async-done | bytes 2097184 | tf_op jit(solution)/shard_map/all_to_all | solution.py:82
  494.9 58.1 %reduce-scatter.5.cloned.1.call-done = f32[64,2048]{1,0:T(8,128)} async-done(((f32[512,2048]{1,0:T(8,128)}), f32[64,2048]{1,0:T(8,128)}) %reduce-scatter.5.cloned.1.call-update) | async-done | bytes 524304 | tf_op jit(solution)/shard_map/reduce_scatter | solution.py:98
  553.0 1.8 add_convert_fusion
  (56 shorter events, 5.7 us)
Async XLA Ops:
  6.5 34.3 %all-gather.3.cloned.1.call-start = ((), (), s32[]{:S(2)}) async-start(), calls=%async_computation.4 | async-start | bytes 2359296 | tf_op jit(solution)/shard_map/all_gather | solution.py:39
  7.3 246.0 %all-reduce.3.cloned.1.call-start = ((), (), s32[]{:S(2)}) async-start(), calls=%async_computation.5 | async-start | bytes 8388608 | tf_op jit(solution)/shard_map/psum | solution.py:78
  42.9 39.0 %copy-start = (bf16[128,8192]{1,0:T(8,128)(2,1)S(1)}, bf16[128,8192]{1,0:T(8,128)(2,1)}, u32[]{:S(2)}) copy-start(bf16[128,8192]{1,0:T(8,128)(2,1)} %all-gather.3.cloned.1.call-done) | copy-start | bytes 6291460
  81.9 11.6 %slice-start = ((s8[16777216]{0:T(1024)(128)(4,1)}), s8[4194304]{0:T(1024)(128)(4,1)S(1)}, s32[]{:S(2)}) async-start(s8[16777216]{0:T(1024)(128)(4,1)} %bitcast.57), calls=%async_computation.10 | async-start | bytes 8388608
  81.9 11.6 %slice-start.1 = ((s8[16777216]{0:T(1024)(128)(4,1)}), s8[4194304]{0:T(1024)(128)(4,1)S(1)}, s32[]{:S(2)}) async-start(s8[16777216]{0:T(1024)(128)(4,1)} %bitcast.57), calls=%async_computation.11 | async-start | bytes 8388608
  81.9 11.6 %slice-start.2 = ((s8[16777216]{0:T(1024)(128)(4,1)}), s8[4194304]{0:T(1024)(128)(4,1)S(1)}, s32[]{:S(2)}) async-start(s8[16777216]{0:T(1024)(128)(4,1)} %bitcast.57), calls=%async_computation.12 | async-start | bytes 8388608
  92.1 2.2 slice-start.3
  99.1 154.2 %copy-start.1 = (bf16[8192]{0:T(1024)(128)(2,1)S(1)}, bf16[8192]{0:T(1024)(128)(2,1)}, u32[]{:S(2)}) copy-start(bf16[8192]{0:T(1024)(128)(2,1)} %param.14) | copy-start | bytes 49156
  99.2 183.9 %all-reduce.5.cloned.1.call-start = ((), (), s32[]{:S(2)}) async-start(), calls=%async_computation.6 | async-start | bytes 8388608 | tf_op jit(solution)/shard_map/psum | solution.py:78
  253.3 163.1 %reduce-scatter.3.cloned.1.call-start = ((), (), s32[]{:S(2)}) async-start(), calls=%async_computation.7 | async-start | bytes 10485760 | tf_op jit(solution)/shard_map/reduce_scatter | solution.py:89
  283.0 34.5 %slice-start.4 = ((s8[8388608]{0:T(1024)(128)(4,1)}), s8[4194304]{0:T(1024)(128)(4,1)S(1)}, s32[]{:S(2)}) async-start(s8[8388608]{0:T(1024)(128)(4,1)} %bitcast.67), calls=%async_computation.14 | async-start | bytes 8388608
  286.8 30.7 %slice-start.5 = ((s8[8388608]{0:T(1024)(128)(4,1)}), s8[4194304]{0:T(1024)(128)(4,1)S(1)}, s32[]{:S(2)}) async-start(s8[8388608]{0:T(1024)(128)(4,1)} %bitcast.67), calls=%async_computation.15 | async-start | bytes 8388608
  287.7 34.4 %slice-start.6 = ((s8[8388608]{0:T(1024)(128)(4,1)}), s8[4194304]{0:T(1024)(128)(4,1)S(1)}, s32[]{:S(2)}) async-start(s8[8388608]{0:T(1024)(128)(4,1)} %bitcast.69), calls=%async_computation.16 | async-start | bytes 8388608
  317.5 4.6 slice-start.7
  330.5 123.9 %all-gather.5.cloned.1.call-start = ((), (), s32[]{:S(2)}) async-start(), calls=%async_computation.8 | async-start | bytes 2621440 | tf_op jit(solution)/shard_map/all_gather | solution.py:95
  419.1 134.0 %reduce-scatter.5.cloned.1.call-start = ((), (), s32[]{:S(2)}) async-start(), calls=%async_computation.9 | async-start | bytes 4718592 | tf_op jit(solution)/shard_map/reduce_scatter | solution.py:98
  466.4 28.6 %all-to-all-start = ((bf16[128,4,2048]{2,0,1:T(8,128)(2,1)}), bf16[128,4,2048]{2,0,1:T(8,128)(2,1)S(1)}, u32[]{:S(2)}, u32[]{:S(2)}) async-start(bf16[128,4,2048]{2,0,1:T(8,128)(2,1)} %bitcast.59), calls=%async_computation | async-start | bytes 4194304 | tf_op jit(solution)/shard_map/all_to_all | solution.py:82
Sparse Core Ops, SparseCore 0:
  8.9 31.8 all-gather.2
  99.3 153.9 all-reduce.2
  255.8 27.1 all-reduce.4
  330.6 85.7 reduce-scatter.2
  419.2 35.1 all-gather.4
  465.0 87.9 reduce-scatter.4
